TPU v7x, 32 devices: a whole 2x2x4 slice. The times are simulated.
32 devices in a mesh: section: 4 (over y, x), dp: 8 (over z, core).
Axes of the slice: x: 2, y: 2, z: 4, core: 2. Of those that a mesh axis runs over, the one named last changes fastest.
Arguments:
- grads: float32 [4, 8, 64, 4096], P('section', 'dp'), may hold values from -4096 to 4096
- skipped: int32 [8], P('dp'), may hold values from 0 to 24
- master: float32 [4, 64, 4096], P('section', 'dp'), may hold values from -6 to 6
- moment_one: float32 [4, 64, 4096], P('section', 'dp'), may hold values from -6 to 6
- moment_two: float32 [4, 64, 4096], P('section', 'dp'), may hold values from 0.25 to 4
- bounds: int32 [4, 9], P('section'), may hold values from 0 to 64, as said below
- step: int32 [1], replicated, may hold values from 1 to 24
Outputs:
- params: bfloat16 [4, 64, 4096], P('section')
- master_next: float32 [4, 64, 4096], P('section', 'dp')
- moment_one_next: float32 [4, 64, 4096], P('section', 'dp')
- moment_two_next: float32 [4, 64, 4096], P('section', 'dp')
- layer_norms: float32 [4, 8], P('section')
- grad_norm: float32 [1], replicated
Inputs may be any that keep to these rules, and one draw needn't show every extreme that they name: `bounds`: each section's row is strictly increasing, starts at 0 and ends at 64.
All inputs are finite; a program needn't handle non-finite values.
Results may differ from a plain program's by a relative error of at most 0.001.
Values may be sent and summed in bfloat16 or wider, within the bound.
A program may use at most 64 MiB of HBM per device.

v0:
```python
import jax
import jax.numpy as jnp
from jax import lax
from jax.sharding import PartitionSpec as P

MICRO = 32


beta_one = 0.9
beta_two = 0.95
learn_rate = 0.05
weight_decay = 0.1
epsilon = 1e-08


def layer_share(row_squares, bounds, own_rows):
    first_row = lax.axis_index("dp") * own_rows
    row_index = first_row + jnp.arange(own_rows, dtype=jnp.int32)
    inside = (row_index[:, None] >= bounds[0, None, :-1]) & (
        row_index[:, None] < bounds[0, None, 1:]
    )
    return jnp.sum(row_squares[:, None] * inside.astype(jnp.float32), axis=0)


def on_device(grads, skipped, master, moment_one, moment_two, bounds, step):
    flat_grads = grads[0, 0]
    rows_all = flat_grads.shape[0]
    width = flat_grads.shape[1]
    own_rows = master.shape[1]
    n_section = lax.axis_size("section")
    summed = lax.psum_scatter(flat_grads, "dp", scatter_dimension=0, tiled=True)
    good_count = (MICRO - skipped[0]).astype(jnp.float32)
    total_good = lax.psum(good_count, "dp")
    mean_grad = summed / total_good
    layer_part = layer_share(jnp.sum(mean_grad * mean_grad, axis=1), bounds, own_rows)
    layer_sq = lax.psum(layer_part, "dp")
    total_sq = lax.psum(jnp.sum(layer_sq), "section")
    grad_rms = jnp.sqrt(total_sq / (n_section * rows_all * width))
    layer_rows = (bounds[0, 1:] - bounds[0, :-1]).astype(jnp.float32)
    layer_norms = jnp.sqrt(layer_sq / (layer_rows * width))
    clipped = mean_grad / jnp.maximum(1.0, grad_rms)
    first_next = beta_one * moment_one[0] + (1.0 - beta_one) * clipped
    second_next = beta_two * moment_two[0] + (1.0 - beta_two) * clipped * clipped
    step_value = step[0].astype(jnp.float32)
    fix_one = 1.0 - jnp.power(beta_one, step_value)
    fix_two = 1.0 - jnp.power(beta_two, step_value)
    update = first_next / fix_one / (jnp.sqrt(second_next / fix_two) + epsilon)
    master_next = master[0] - learn_rate * (update + weight_decay * master[0])
    gathered = lax.all_gather(master_next.astype(jnp.bfloat16), "dp", axis=0, tiled=True)
    return (
        gathered[None],
        master_next[None],
        first_next[None],
        second_next[None],
        layer_norms[None],
        grad_rms.reshape(1),
    )


def solution(mesh):
    in_specs = (
        P("section", "dp", None, None),
        P("dp"),
        P("section", "dp", None),
        P("section", "dp", None),
        P("section", "dp", None),
        P("section", None),
        P(),
    )
    out_specs = (
        P("section", None, None),
        P("section", "dp", None),
        P("section", "dp", None),
        P("section", "dp", None),
        P("section", None),
        P(),
    )
    return jax.shard_map(
        on_device, mesh=mesh, in_specs=in_specs, out_specs=out_specs, check_vma=False
    )
```

profile of v0, /device:TPU:0, one launch (start us, length us, event | category | flops | bytes accessed | tf_op | source)
XLA Modules:
  0.0 99.1 jit_solution(8296331558367026097)
XLA Ops:
  7.2 0.0 reduce-scatter.2.cloned.1.call-start
  7.2 0.0 copy-start.1
  7.2 0.0 copy-start.2
  7.2 0.0 copy-start.3
  7.2 0.7 reduce-scatter.2.cloned.1.call-update
  8.5 19.4 %psum.21 = f32[]{:T(128)} all-reduce(f32[]{:T(128)} %bitcast.3), channel_id=1, replica_groups=mesh['section'=4,'dp'=8] {'dp'}, use_global_device_ids=true, to_apply=%region_1.0 | all-reduce | flops 1 | bytes 8 | tf_op jit(solution)/shard_map/psum | solution.py:33
  28.7 0.0 copy-start.4
  28.7 0.6 copy-done.4
  29.3 0.1 slice_bitcast_fusion.1
  29.4 16.2 %reduce-scatter.2.cloned.1.call-done = f32[8,4096]{1,0:T(8,128)} async-done(((f32[64,4096]{1,0:T(8,128)}), f32[8,4096]{1,0:T(8,128)}) %reduce-scatter.2.cloned.1.call-update) | async-done | bytes 131088 | tf_op jit(solution)/shard_map/reduce_scatter | solution.py:31
  45.7 0.0 copy-start
  45.7 1.7 %multiply_reduce_fusion = f32[8]{0:T(128)S(1)} fusion(f32[8,4096]{1,0:T(8,128)} %reduce-scatter.2.cloned.1.call-done, f32[]{:T(128)} %psum.21), kind=kLoop, calls=%fused_computation.7 | loop fusion | flops 98296 | bytes 131108 | tf_op jit(solution)/shard_map/reduce_sum | solution.py:35
  47.4 0.1 select_reduce_fusion
  47.5 13.7 %psum.22 = f32[8]{0:T(128)S(1)} all-reduce(f32[8]{0:T(128)S(1)} %select_reduce_fusion), channel_id=1, replica_groups=mesh['section'=4,'dp'=8] {'dp'}, use_global_device_ids=true, to_apply=%region_4.0 | all-reduce | flops 8 | bytes 64 | tf_op jit(solution)/shard_map/psum | solution.py:36
  61.2 1.2 %sqrt_bitcast_fusion = (f32[1,8]{1,0:T(1,128)}, f32[]{:T(128)}) fusion(f32[8]{0:T(128)S(1)} %psum.22, s32[1,9]{1,0:T(1,128)S(1)} %copy-done.4), kind=kLoop, calls=%fused_computation.10 | loop fusion | flops 39 | bytes 132 | tf_op jit(solution)/shard_map/broadcast_in_dim | solution.py:55
  62.4 10.8 %psum.23 = f32[]{:T(128)} all-reduce(f32[]{:T(128)} %get-tuple-element.11), channel_id=1, replica_groups=mesh['section'=4,'dp'=8] {'section'}, use_global_device_ids=true, to_apply=%region_6.0 | all-reduce | flops 1 | bytes 8 | tf_op jit(solution)/shard_map/psum | solution.py:37
  74.6 0.0 copy-done.1
  74.6 0.0 copy-done.2
  74.6 0.0 copy-done.3
  74.6 0.0 copy-done
  74.6 0.8 fusion.5
  75.4 14.9 %all_gather.3 = bf16[64,4096]{1,0:T(8,128)(2,1)S(1)} all-gather(bf16[8,4096]{1,0:T(8,128)(2,1)S(1)} %get-tuple-element.6), channel_id=1, replica_groups=mesh['section'=4,'dp'=8] {'dp'}, dimensions={0}, use_global_device_ids=true | all-gather | bytes 589824 | tf_op jit(solution)/shard_map/all_gather | solution.py:49
  90.4 0.8 copy.16
  (1 shorter events, 0.0 us)
Async XLA Ops:
  7.2 38.5 %reduce-scatter.2.cloned.1.call-start = ((), (), s32[]{:S(2)}) async-start(), calls=%async_computation.1 | async-start | bytes 1179648 | tf_op jit(solution)/shard_map/reduce_scatter | solution.py:31
  7.2 67.4 %copy-start.1 = (f32[1,8,4096]{2,1,0:T(8,128)S(1)}, f32[1,8,4096]{2,1,0:T(8,128)}, u32[]{:S(2)}) copy-start(f32[1,8,4096]{2,1,0:T(8,128)} %param.11) | copy-start | bytes 393220
  7.2 67.4 %copy-start.2 = (f32[1,8,4096]{2,1,0:T(8,128)S(1)}, f32[1,8,4096]{2,1,0:T(8,128)}, u32[]{:S(2)}) copy-start(f32[1,8,4096]{2,1,0:T(8,128)} %param.10) | copy-start | bytes 393220
  7.2 67.4 %copy-start.3 = (f32[1,8,4096]{2,1,0:T(8,128)S(1)}, f32[1,8,4096]{2,1,0:T(8,128)}, u32[]{:S(2)}) copy-start(f32[1,8,4096]{2,1,0:T(8,128)} %param.9) | copy-start | bytes 393220
  28.7 0.7 copy-start.4
  45.7 29.0 %copy-start = (f32[8,4096]{1,0:T(8,128)S(1)}, f32[8,4096]{1,0:T(8,128)}, u32[]{:S(2)}) copy-start(f32[8,4096]{1,0:T(8,128)} %reduce-scatter.2.cloned.1.call-done) | copy-start | bytes 393220
Sparse Core Ops, SparseCore 0:
  10.2 35.3 reduce-scatter.1
where the time goes:
time: 99.4 us; the launch traced here: 99.1 us
  blocking collectives  58.9 us (59%)
  between operations  18 us (18%)
  waiting for transfers between devices  16.9 us (17%)
  other arithmetic  3.83 us (4%)
  local copies, waits for them, and re-layouts  1.52 us (2%)
    psum x1, blocking collectives, on_device(): total_good = lax.psum(good_count, 'dp')  19.4 us
    reduce_scatter x1, waiting for transfers between devices, on_device(): summed = lax.psum_scatter(flat_grads, 'dp', scatter_dimension=0, tiled=True)  16.2 us
    all_gather x1, blocking collectives, on_device(): lax.all_gather(master_next.astype(jnp.bfloat16), 'dp', axis=0, tiled=True)  14.9 us
    psum x1, blocking collectives, on_device(): layer_sq = lax.psum(layer_part, 'dp')  13.7 us
    psum x1, blocking collectives, on_device(): total_sq = lax.psum(jnp.sum(layer_sq), 'section')  10.8 us
  transfers between devices with their start and end apart: 1, of which 1 were waited for; matrix products, arithmetic and copies ran while one was open for 0% of the time, Pallas kernels for 0%

commit v1 on v0

v1 whole, which is shorter than its diff:
```python
import functools
import math

import jax
import jax.numpy as jnp
from jax import lax
from jax.experimental import pallas as pl
from jax.experimental.pallas import tpu as pltpu
from jax.sharding import PartitionSpec as P

MICRO = 32
PAIR = 2

beta_one = 0.9
beta_two = 0.95
learn_rate = 0.05
weight_decay = 0.1
epsilon = 1e-08

MESH = pl.DeviceIdType.MESH
LANES = 128


def repeat(count, body):
    if count <= 8:
        for index in range(count):
            body(index)
    else:
        lax.fori_loop(0, count, lambda index, _: (body(index), None)[1], None)


def kernel(
    n_section,
    n_dp,
    layers,
    grads,
    skipped,
    master,
    moment_one,
    moment_two,
    bounds,
    step,
    params,
    master_next,
    first_next,
    second_next,
    layer_norms,
    grad_norm,
    mine,
    theirs,
    paired,
    outgoing,
    incoming,
    dp_stats,
    section_stats,
    state,
    result,
    load_sem,
    pair_send,
    pair_recv,
    sum_send,
    sum_recv,
    stat_send,
    stat_recv,
    sec_send,
    sec_recv,
    row_send,
    row_recv,
    near_send,
    near_recv,
    store_sem,
):
    section = lax.axis_index("section")
    me = lax.axis_index("dp")
    n_chip = n_dp // PAIR
    chip, core = me // PAIR, lax.rem(me, PAIR)
    other = 1 - core
    partner = chip * PAIR + other
    own_rows, width = mine.shape[1], mine.shape[2]
    rows_all = n_dp * own_rows

    def remote(src, dst, send, recv, sec, dp):
        return pltpu.make_async_remote_copy(
            src_ref=src, dst_ref=dst, send_sem=send, recv_sem=recv,
            device_id=(sec, dp), device_id_type=MESH,
        )

    load_theirs = pltpu.make_async_copy(grads.at[:, other], theirs, load_sem.at[0])
    load_mine = pltpu.make_async_copy(grads.at[:, core], mine, load_sem.at[1])
    load_theirs.start()
    load_mine.start()
    state_loads = [
        pltpu.make_async_copy(source, state.at[k], load_sem.at[2 + k])
        for k, source in enumerate((master, moment_one, moment_two))
    ]
    for load in state_loads:
        load.start()

    barrier = pltpu.get_barrier_semaphore()

    def greet_dp(k):
        pl.semaphore_signal(
            barrier, inc=1, device_id=(section, lax.rem(me + k + 1, n_dp)), device_id_type=MESH
        )

    def greet_section(k):
        pl.semaphore_signal(
            barrier, inc=1, device_id=(lax.rem(section + k + 1, n_section), me), device_id_type=MESH
        )

    repeat(n_dp - 1, greet_dp)
    repeat(n_section - 1, greet_section)
    pl.semaphore_wait(barrier, n_dp + n_section - 2)

    def pair_copy(off):
        z = lax.rem(chip + off, n_chip)
        return remote(
            theirs.at[z], paired.at[z], pair_send.at[off], pair_recv.at[off], section, partner
        )

    def order(k):
        return k + 1 if isinstance(k, int) and k + 1 < n_chip else lax.rem(k + 1, n_chip)

    load_theirs.wait()
    repeat(n_chip, lambda k: pair_copy(order(k)).start())
    load_mine.wait()

    def sum_copy(k):
        z = lax.rem(chip + k + 1, n_chip)
        return remote(
            outgoing.at[k], incoming.at[k], sum_send.at[k], sum_recv.at[k], section, z * PAIR + core
        )

    def send_sum(k):
        z = lax.rem(chip + k + 1, n_chip)
        pair_copy(k + 1).wait_recv()
        outgoing[k] = (mine[z] + paired[z]).astype(jnp.bfloat16)
        sum_copy(k).start()

    repeat(n_chip - 1, send_sum)
    pair_copy(0).wait_recv()
    mine[chip] = mine[chip] + paired[chip]

    def take_sum(k):
        sum_copy(k).wait_recv()
        mine[chip] = mine[chip] + incoming[k].astype(jnp.float32)

    repeat(n_chip - 1, take_sum)
    total_grad = mine[chip]

    row_squares = jnp.sum(total_grad * total_grad, axis=1, keepdims=True)
    row = me * own_rows + lax.broadcasted_iota(jnp.int32, (own_rows, LANES), 0)
    lane = lax.broadcasted_iota(jnp.int32, (1, LANES), 1)
    low = jnp.zeros((1, LANES), jnp.int32)
    high = jnp.zeros((1, LANES), jnp.int32)
    for layer in range(layers):
        low = jnp.where(lane == layer, bounds[0, layer], low)
        high = jnp.where(lane == layer, bounds[0, layer + 1], high)
    inside = (row >= low) & (row < high)
    own_stats = jnp.sum(jnp.where(inside, row_squares, 0.0), axis=0, keepdims=True)
    good = (MICRO - skipped[0]).astype(jnp.float32)
    dp_stats[me] = jnp.where(lane == layers, good, own_stats)

    def stat_copy(k):
        return remote(
            dp_stats.at[me], dp_stats.at[me], stat_send.at[k], stat_recv.at[k],
            section, lax.rem(me + k + 1, n_dp),
        )

    repeat(n_dp - 1, lambda k: stat_copy(k).start())
    for load in state_loads:
        load.wait()
    step_value = jnp.full((1, 1), step[0], jnp.int32).astype(jnp.float32)
    fix_one = 1.0 - jnp.exp(step_value * math.log(beta_one))
    fix_two = 1.0 - jnp.exp(step_value * math.log(beta_two))
    repeat(n_dp - 1, lambda k: stat_copy(k).wait_recv())
    section_sum = jnp.sum(dp_stats[...], axis=0)
    section_stats[section] = section_sum

    def section_copy(k):
        return remote(
            section_stats.at[section], section_stats.at[section], sec_send.at[k], sec_recv.at[k],
            lax.rem(section + k + 1, n_section), me,
        )

    repeat(n_section - 1, lambda k: section_copy(k).start())
    total_good = jnp.sum(jnp.where(lane == layers, section_sum, 0.0), axis=1, keepdims=True)
    layer_rows = jnp.where(lane < layers, high - low, 1).astype(jnp.float32)
    norms = jnp.sqrt(section_sum / (layer_rows * width)) / total_good
    layer_norms[...] = norms[:, :layers]
    repeat(n_section - 1, lambda k: section_copy(k).wait_recv())
    everything = jnp.sum(section_stats[...], axis=0)
    total_sq = jnp.sum(jnp.where(lane < layers, everything, 0.0), axis=1, keepdims=True)
    grad_rms = jnp.sqrt(total_sq / (n_section * rows_all * width)) / total_good
    grad_norm[...] = grad_rms

    clipped = total_grad * (1.0 / (total_good * jnp.maximum(1.0, grad_rms)))
    one = beta_one * state[1] + (1.0 - beta_one) * clipped
    two = beta_two * state[2] + (1.0 - beta_two) * clipped * clipped
    update = one * (1.0 / fix_one) / (jnp.sqrt(two * (1.0 / fix_two)) + epsilon)
    master_new = state[0] - learn_rate * (update + weight_decay * state[0])
    params[me] = master_new.astype(jnp.bfloat16)

    def near_copy(off):
        block = lax.rem(chip + off, n_chip) * PAIR + core
        return remote(
            params.at[block], params.at[block], near_send.at[off], near_recv.at[off], section, partner
        )

    def row_copy(k):
        return remote(
            params.at[me], params.at[me], row_send.at[k], row_recv.at[k],
            section, lax.rem(chip + k + 1, n_chip) * PAIR + core,
        )

    repeat(n_chip - 1, lambda k: row_copy(k).start())
    near_copy(0).start()
    result[0] = master_new
    result[1] = one
    result[2] = two
    stores = [
        pltpu.make_async_copy(result.at[k], target, store_sem.at[k])
        for k, target in enumerate((master_next, first_next, second_next))
    ]
    for store in stores:
        store.start()

    def pass_on(k):
        row_copy(k).wait_recv()
        near_copy(n_chip - 1 - k).start()

    repeat(n_chip - 1, pass_on)
    repeat(n_chip, lambda k: near_copy(k).wait_recv())
    for store in stores:
        store.wait()
    repeat(n_chip, lambda k: pair_copy(k).wait_send())
    repeat(n_chip - 1, lambda k: sum_copy(k).wait_send())
    repeat(n_dp - 1, lambda k: stat_copy(k).wait_send())
    repeat(n_section - 1, lambda k: section_copy(k).wait_send())
    repeat(n_chip - 1, lambda k: row_copy(k).wait_send())
    repeat(n_chip, lambda k: near_copy(k).wait_send())


def on_device(n_section, n_dp, grads, skipped, master, moment_one, moment_two, bounds, step):
    rows_all, width = grads.shape[2:]
    own_rows = master.shape[1]
    layers = bounds.shape[1] - 1
    n_chip = n_dp // PAIR
    any_space = pl.BlockSpec(memory_space=pl.ANY)
    smem = pl.BlockSpec(memory_space=pltpu.SMEM)
    vmem = pl.BlockSpec(memory_space=pltpu.VMEM)
    own = jax.ShapeDtypeStruct((own_rows, width), jnp.float32)
    dma = pltpu.SemaphoreType.DMA
    blocks = pltpu.VMEM((n_chip, own_rows, width), jnp.float32)
    halves = pltpu.VMEM((n_chip - 1, own_rows, width), jnp.bfloat16)
    params, master_next, first_next, second_next, layer_norms, grad_norm = pl.pallas_call(
        functools.partial(kernel, n_section, n_dp, layers),
        out_shape=(
            jax.ShapeDtypeStruct((n_dp, own_rows, width), jnp.bfloat16),
            own,
            own,
            own,
            jax.ShapeDtypeStruct((1, layers), jnp.float32),
            jax.ShapeDtypeStruct((1, 1), jnp.float32),
        ),
        in_specs=[any_space, smem, any_space, any_space, any_space, smem, smem],
        out_specs=(vmem, any_space, any_space, any_space, vmem, vmem),
        scratch_shapes=[
            blocks,
            blocks,
            blocks,
            halves,
            halves,
            pltpu.VMEM((n_dp, 1, LANES), jnp.float32),
            pltpu.VMEM((n_section, 1, LANES), jnp.float32),
            pltpu.VMEM((3, own_rows, width), jnp.float32),
            pltpu.VMEM((3, own_rows, width), jnp.float32),
            dma((5,)),
            dma((n_chip,)),
            dma((n_chip,)),
            dma((n_chip - 1,)),
            dma((n_chip - 1,)),
            dma((n_dp - 1,)),
            dma((n_dp - 1,)),
            dma((n_section - 1,)),
            dma((n_section - 1,)),
            dma((n_chip - 1,)),
            dma((n_chip - 1,)),
            dma((n_chip,)),
            dma((n_chip,)),
            dma((3,)),
        ],
        compiler_params=pltpu.CompilerParams(collective_id=0, has_side_effects=True),
    )(
        grads.reshape(n_chip, PAIR, own_rows, width),
        skipped,
        master[0],
        moment_one[0],
        moment_two[0],
        bounds,
        step,
    )
    return (
        params.reshape(1, rows_all, width),
        master_next[None],
        first_next[None],
        second_next[None],
        layer_norms,
        grad_norm.reshape(1),
    )


def solution(mesh):
    in_specs = (
        P("section", "dp", None, None),
        P("dp"),
        P("section", "dp", None),
        P("section", "dp", None),
        P("section", "dp", None),
        P("section", None),
        P(),
    )
    out_specs = (
        P("section", None, None),
        P("section", "dp", None),
        P("section", "dp", None),
        P("section", "dp", None),
        P("section", None),
        P(),
    )
    body = functools.partial(on_device, mesh.shape["section"], mesh.shape["dp"])
    return jax.shard_map(
        body, mesh=mesh, in_specs=in_specs, out_specs=out_specs, check_vma=False
    )
```

time: 99.4 us -> 38.5 us (0.39)
  blocking collectives: 58.9 us -> 0 us
  Pallas kernels: 0 us -> 29.7 us
  waiting for transfers between devices: 16.9 us -> 0 us
  between operations: 18 us -> 3.63 us
  other arithmetic: 3.83 us -> 0 us
  local copies, waits for them, and re-layouts: 1.52 us -> 4.98 us
    psum x3 -> x0, blocking collectives: 44 us -> none  [the longest x1 19.4 us: on_device(): total_good = lax.psum(good_count, 'dp')]
    pallas_call x0 -> x1, Pallas kernels: none -> 29.7 us  [on_device(): pl.pallas_call(functools.partial(kernel, n_section, n_dp, layers), out_sh...]
    reduce_scatter x1 -> x0, waiting for transfers between devices: 16.2 us -> none  [on_device(): summed = lax.psum_scatter(flat_grads, 'dp', scatter_dimension=0, tiled=True)]
    all_gather x1 -> x0, blocking collectives: 14.9 us -> none  [on_device(): lax.all_gather(master_next.astype(jnp.bfloat16), 'dp', axis=0, tiled=True)]
    unnamed x11 -> x13, local copies, waits for them, and re-layouts: 1.45 us -> 4.98 us
    reduce_sum x2 -> x0, other arithmetic: 1.82 us -> none  [the longest x1 1.73 us: on_device(): jnp.sum(mean_grad * mean_grad, axis=1)]
    broadcast_in_dim x1 -> x0, other arithmetic: 1.2 us -> none  [on_device(): layer_norms[None]]
  transfers between devices with their start and end apart: 1 -> 0, of which waited for: 1 -> 0; matrix products, arithmetic and copies ran while one was open for 0% -> 0% of each run, Pallas kernels for 0% -> 0%
where the time goes in v1:
time: 38.5 us; the launch traced here: 38.3 us
  Pallas kernels  29.7 us (77%)
  local copies, waits for them, and re-layouts  4.98 us (13%)
  between operations  3.63 us (9%)
    pallas_call x1, Pallas kernels, on_device(): pl.pallas_call(functools.partial(kernel, n_section, n_dp, layers), out_sh...  29.7 us
    unnamed x13, local copies, waits for them, and re-layouts  4.98 us

profile of v1, /device:TPU:0, one launch (start us, length us, event | category | flops | bytes accessed | tf_op | source)
XLA Modules:
  0.0 38.3 jit_solution(6775532520059292156)
XLA Ops:
  1.9 29.7 %shard_map.118 = (bf16[8,8,4096]{2,1,0:T(8,128)(2,1)}, f32[8,4096]{1,0:T(8,128)}, f32[8,4096]{1,0:T(8,128)}, f32[8,4096]{1,0:T(8,128)}, f32[1,8]{1,0:T(1,128)}, /*index=5*/f32[1,1]{1,0:T(1,128)}) custom-call(f32[4,2,8,4096]{3,2,1,0:T(8,128)} %bitcast.9, s32[1]{0:T(128)S(6)} %copy.19.skipped, f32[8,4096]{1,0:T(8,128)} %bitcast.11, f32[8,4096]{1,0:T(8,128)} %bitcast.12, ...), custom_call_target="tpu_custom_call" | custom-call | tf_op jit(solution)/shard_map/pallas_call | solution.py:256
  31.6 0.0 copy-start.2
  31.6 1.9 %copy.21 = bf16[1,64,4096]{2,1,0:T(8,128)(2,1)} copy(bf16[1,64,4096]{2,1,0:T(8,128)(2,1)} %bitcast.10) | data formatting | bytes 1048576
  33.5 0.0 copy-done.2
  33.6 0.0 copy-start.1
  33.6 0.7 %copy.22 = f32[1,8,4096]{2,1,0:T(8,128)} copy(f32[1,8,4096]{2,1,0:T(8,128)S(1)} %bitcast.16) | data formatting | bytes 262144
  34.2 0.3 copy-done.1
  34.5 0.0 copy-start
  34.5 0.7 %copy.23 = f32[1,8,4096]{2,1,0:T(8,128)} copy(f32[1,8,4096]{2,1,0:T(8,128)S(1)} %bitcast.15) | data formatting | bytes 262144
  35.2 0.3 copy-done
  35.5 0.0 copy-start.3
  35.5 0.7 %copy.24 = f32[1,8,4096]{2,1,0:T(8,128)} copy(f32[1,8,4096]{2,1,0:T(8,128)S(1)} %bitcast.14) | data formatting | bytes 262144
  36.1 0.0 copy-done.3
  36.1 0.5 %copy.25 = f32[1,8]{1,0:T(1,128)} copy(f32[1,8]{1,0:T(1,128)S(1)} %copy-done.3) | data formatting | bytes 64
Async XLA Ops:
  31.6 1.9 %copy-start.2 = (f32[8,4096]{1,0:T(8,128)S(1)}, f32[8,4096]{1,0:T(8,128)}, u32[]{:S(2)}) copy-start(f32[8,4096]{1,0:T(8,128)} %get-tuple-element.13) | copy-start | bytes 393220
  33.6 1.0 %copy-start.1 = (f32[8,4096]{1,0:T(8,128)S(1)}, f32[8,4096]{1,0:T(8,128)}, u32[]{:S(2)}) copy-start(f32[8,4096]{1,0:T(8,128)} %get-tuple-element.14) | copy-start | bytes 393220
  34.5 1.0 %copy-start = (f32[8,4096]{1,0:T(8,128)S(1)}, f32[8,4096]{1,0:T(8,128)}, u32[]{:S(2)}) copy-start(f32[8,4096]{1,0:T(8,128)} %get-tuple-element.15) | copy-start | bytes 393220
  35.5 0.7 %copy-start.3 = (f32[1,8]{1,0:T(1,128)S(1)}, f32[1,8]{1,0:T(1,128)}, u32[]{:S(2)}) copy-start(f32[1,8]{1,0:T(1,128)} %get-tuple-element.28) | copy-start | bytes 100

commit v2 on v1

--- a/solution.py
+++ b/solution.py
@@ -19,6 +19,9 @@
 
 MESH = pl.DeviceIdType.MESH
 LANES = 128
+SLACK = 2**20
+SPARE = 2**14
+VMEM_BYTES = 67043328
 
 
 def repeat(count, body):
@@ -34,18 +37,14 @@
     n_dp,
     layers,
     grads,
-    skipped,
+    counts,
     master,
     moment_one,
     moment_two,
     bounds,
-    step,
     params,
-    master_next,
-    first_next,
-    second_next,
-    layer_norms,
-    grad_norm,
+    result,
+    norms_out,
     mine,
     theirs,
     paired,
@@ -54,7 +53,8 @@
     dp_stats,
     section_stats,
     state,
-    result,
+    counts_in,
+    bounds_in,
     load_sem,
     pair_send,
     pair_recv,
@@ -68,7 +68,6 @@
     row_recv,
     near_send,
     near_recv,
-    store_sem,
 ):
     section = lax.axis_index("section")
     me = lax.axis_index("dp")
@@ -85,6 +84,20 @@
             device_id=(sec, dp), device_id_type=MESH,
         )
 
+    barrier = pltpu.get_barrier_semaphore()
+
+    def greet_dp(k):
+        pl.semaphore_signal(
+            barrier, inc=1, device_id=(section, lax.rem(me + k + 1, n_dp)), device_id_type=MESH
+        )
+
+    def greet_section(k):
+        pl.semaphore_signal(
+            barrier, inc=1, device_id=(lax.rem(section + k + 1, n_section), me), device_id_type=MESH
+        )
+
+    repeat(n_dp - 1, greet_dp)
+    repeat(n_section - 1, greet_section)
     load_theirs = pltpu.make_async_copy(grads.at[:, other], theirs, load_sem.at[0])
     load_mine = pltpu.make_async_copy(grads.at[:, core], mine, load_sem.at[1])
     load_theirs.start()
@@ -93,23 +106,15 @@
         pltpu.make_async_copy(source, state.at[k], load_sem.at[2 + k])
         for k, source in enumerate((master, moment_one, moment_two))
     ]
+    state_loads += [
+        pltpu.make_async_copy(source, target, load_sem.at[5 + k])
+        for k, (source, target) in enumerate(
+            ((counts, counts_in), (bounds, bounds_in))
+        )
+    ]
     for load in state_loads:
         load.start()
 
-    barrier = pltpu.get_barrier_semaphore()
-
-    def greet_dp(k):
-        pl.semaphore_signal(
-            barrier, inc=1, device_id=(section, lax.rem(me + k + 1, n_dp)), device_id_type=MESH
-        )
-
-    def greet_section(k):
-        pl.semaphore_signal(
-            barrier, inc=1, device_id=(lax.rem(section + k + 1, n_section), me), device_id_type=MESH
-        )
-
-    repeat(n_dp - 1, greet_dp)
-    repeat(n_section - 1, greet_section)
     pl.semaphore_wait(barrier, n_dp + n_section - 2)
 
     def pair_copy(off):
@@ -148,17 +153,19 @@
     repeat(n_chip - 1, take_sum)
     total_grad = mine[chip]
 
+    for load in state_loads:
+        load.wait()
     row_squares = jnp.sum(total_grad * total_grad, axis=1, keepdims=True)
     row = me * own_rows + lax.broadcasted_iota(jnp.int32, (own_rows, LANES), 0)
     lane = lax.broadcasted_iota(jnp.int32, (1, LANES), 1)
     low = jnp.zeros((1, LANES), jnp.int32)
     high = jnp.zeros((1, LANES), jnp.int32)
     for layer in range(layers):
-        low = jnp.where(lane == layer, bounds[0, layer], low)
-        high = jnp.where(lane == layer, bounds[0, layer + 1], high)
+        low = jnp.where(lane == layer, bounds_in[0, layer], low)
+        high = jnp.where(lane == layer, bounds_in[0, layer + 1], high)
     inside = (row >= low) & (row < high)
     own_stats = jnp.sum(jnp.where(inside, row_squares, 0.0), axis=0, keepdims=True)
-    good = (MICRO - skipped[0]).astype(jnp.float32)
+    good = (MICRO - counts_in[0, 0]).astype(jnp.float32)
     dp_stats[me] = jnp.where(lane == layers, good, own_stats)
 
     def stat_copy(k):
@@ -168,9 +175,7 @@
         )
 
     repeat(n_dp - 1, lambda k: stat_copy(k).start())
-    for load in state_loads:
-        load.wait()
-    step_value = jnp.full((1, 1), step[0], jnp.int32).astype(jnp.float32)
+    step_value = jnp.full((1, 1), counts_in[0, 1], jnp.int32).astype(jnp.float32)
     fix_one = 1.0 - jnp.exp(step_value * math.log(beta_one))
     fix_two = 1.0 - jnp.exp(step_value * math.log(beta_two))
     repeat(n_dp - 1, lambda k: stat_copy(k).wait_recv())
@@ -187,12 +192,12 @@
     total_good = jnp.sum(jnp.where(lane == layers, section_sum, 0.0), axis=1, keepdims=True)
     layer_rows = jnp.where(lane < layers, high - low, 1).astype(jnp.float32)
     norms = jnp.sqrt(section_sum / (layer_rows * width)) / total_good
-    layer_norms[...] = norms[:, :layers]
+    norms_out[0] = norms
     repeat(n_section - 1, lambda k: section_copy(k).wait_recv())
     everything = jnp.sum(section_stats[...], axis=0)
     total_sq = jnp.sum(jnp.where(lane < layers, everything, 0.0), axis=1, keepdims=True)
     grad_rms = jnp.sqrt(total_sq / (n_section * rows_all * width)) / total_good
-    grad_norm[...] = grad_rms
+    norms_out[1] = jnp.broadcast_to(grad_rms, (1, LANES))
 
     clipped = total_grad * (1.0 / (total_good * jnp.maximum(1.0, grad_rms)))
     one = beta_one * state[1] + (1.0 - beta_one) * clipped
@@ -218,12 +223,6 @@
     result[0] = master_new
     result[1] = one
     result[2] = two
-    stores = [
-        pltpu.make_async_copy(result.at[k], target, store_sem.at[k])
-        for k, target in enumerate((master_next, first_next, second_next))
-    ]
-    for store in stores:
-        store.start()
 
     def pass_on(k):
         row_copy(k).wait_recv()
@@ -231,8 +230,6 @@
 
     repeat(n_chip - 1, pass_on)
     repeat(n_chip, lambda k: near_copy(k).wait_recv())
-    for store in stores:
-        store.wait()
     repeat(n_chip, lambda k: pair_copy(k).wait_send())
     repeat(n_chip - 1, lambda k: sum_copy(k).wait_send())
     repeat(n_dp - 1, lambda k: stat_copy(k).wait_send())
@@ -241,30 +238,41 @@
     repeat(n_chip, lambda k: near_copy(k).wait_send())
 
 
+def write_out(params, result, norms, params_out, master_next, first_next, second_next, layer_norms, grad_norm, sem):
+    copies = [pltpu.make_async_copy(params, params_out, sem.at[3])]
+    copies += [
+        pltpu.make_async_copy(result.at[k], target, sem.at[k])
+        for k, target in enumerate((master_next, first_next, second_next))
+    ]
+    for copy in copies:
+        copy.start()
+    layer_norms[...] = norms[0][:, : layer_norms.shape[1]]
+    grad_norm[...] = norms[1][:, :1]
+    for copy in copies:
+        copy.wait()
+
+
 def on_device(n_section, n_dp, grads, skipped, master, moment_one, moment_two, bounds, step):
     rows_all, width = grads.shape[2:]
     own_rows = master.shape[1]
     layers = bounds.shape[1] - 1
     n_chip = n_dp // PAIR
-    any_space = pl.BlockSpec(memory_space=pl.ANY)
-    smem = pl.BlockSpec(memory_space=pltpu.SMEM)
+    hbm = pl.BlockSpec(memory_space=pltpu.HBM)
+    held_bytes = rows_all * width * 2 + 3 * own_rows * width * 4 + SPARE
     vmem = pl.BlockSpec(memory_space=pltpu.VMEM)
     own = jax.ShapeDtypeStruct((own_rows, width), jnp.float32)
     dma = pltpu.SemaphoreType.DMA
     blocks = pltpu.VMEM((n_chip, own_rows, width), jnp.float32)
     halves = pltpu.VMEM((n_chip - 1, own_rows, width), jnp.bfloat16)
-    params, master_next, first_next, second_next, layer_norms, grad_norm = pl.pallas_call(
+    held = pl.pallas_call(
         functools.partial(kernel, n_section, n_dp, layers),
         out_shape=(
-            jax.ShapeDtypeStruct((n_dp, own_rows, width), jnp.bfloat16),
-            own,
-            own,
-            own,
-            jax.ShapeDtypeStruct((1, layers), jnp.float32),
-            jax.ShapeDtypeStruct((1, 1), jnp.float32),
+            pltpu.VMEM((n_dp, own_rows, width), jnp.bfloat16),
+            pltpu.VMEM((3, own_rows, width), jnp.float32),
+            pltpu.VMEM((2, 1, LANES), jnp.float32),
         ),
-        in_specs=[any_space, smem, any_space, any_space, any_space, smem, smem],
-        out_specs=(vmem, any_space, any_space, any_space, vmem, vmem),
+        in_specs=[hbm] * 6,
+        out_specs=(vmem, vmem, vmem),
         scratch_shapes=[
             blocks,
             blocks,
@@ -274,8 +282,9 @@
             pltpu.VMEM((n_dp, 1, LANES), jnp.float32),
             pltpu.VMEM((n_section, 1, LANES), jnp.float32),
             pltpu.VMEM((3, own_rows, width), jnp.float32),
-            pltpu.VMEM((3, own_rows, width), jnp.float32),
-            dma((5,)),
+            pltpu.SMEM((1, 2), jnp.int32),
+            pltpu.SMEM(bounds.shape, jnp.int32),
+            dma((7,)),
             dma((n_chip,)),
             dma((n_chip,)),
             dma((n_chip - 1,)),
@@ -288,18 +297,33 @@
             dma((n_chip - 1,)),
             dma((n_chip,)),
             dma((n_chip,)),
-            dma((3,)),
         ],
-        compiler_params=pltpu.CompilerParams(collective_id=0, has_side_effects=True),
+        compiler_params=pltpu.CompilerParams(
+            collective_id=0, has_side_effects=True, vmem_limit_bytes=VMEM_BYTES - held_bytes
+        ),
     )(
         grads.reshape(n_chip, PAIR, own_rows, width),
-        skipped,
+        jnp.concatenate((skipped, step))[None],
         master[0],
         moment_one[0],
         moment_two[0],
         bounds,
-        step,
-    )
+    )
+    params, master_next, first_next, second_next, layer_norms, grad_norm = pl.pallas_call(
+        write_out,
+        out_shape=(
+            jax.ShapeDtypeStruct((n_dp, own_rows, width), jnp.bfloat16),
+            own,
+            own,
+            own,
+            jax.ShapeDtypeStruct((1, layers), jnp.float32),
+            jax.ShapeDtypeStruct((1, 1), jnp.float32),
+        ),
+        in_specs=[vmem] * 3,
+        out_specs=(hbm, hbm, hbm, hbm, vmem, vmem),
+        scratch_shapes=[dma((4,))],
+        compiler_params=pltpu.CompilerParams(vmem_limit_bytes=SLACK),
+    )(*held)
     return (
         params.reshape(1, rows_all, width),
         master_next[None],

time: 38.5 us -> 32.3 us (0.84)
  local copies, waits for them, and re-layouts: 4.98 us -> 0 us
  between operations: 3.63 us -> 1.93 us
  other arithmetic: 0 us -> 0.59 us
    unnamed x13 -> x0, local copies, waits for them, and re-layouts: 4.98 us -> none
    pallas_call x1, Pallas kernels: 29.7 us -> 28.2 us  [on_device(): pl.pallas_call(functools.partial(kernel, n_section, n_dp, layers), out_sh...]
    pallas_call x0 -> x1, Pallas kernels: none -> 1.47 us  [on_device(): pl.pallas_call(write_out, out_shape=(jax.ShapeDtypeStruct((n_dp, own_rows...]
    broadcast_in_dim x0 -> x1, other arithmetic: none -> 0.59 us  [on_device(): jnp.concatenate((skipped, step))[None]]
where the time goes in v2:
time: 32.3 us; the launch traced here: 32.2 us
  Pallas kernels  29.6 us (92%)
  between operations  1.93 us (6%)
  other arithmetic  0.59 us (2%)
    pallas_call x1, Pallas kernels, on_device(): pl.pallas_call(functools.partial(kernel, n_section, n_dp, layers), out_sh...  28.2 us
    pallas_call x1, Pallas kernels, on_device(): pl.pallas_call(write_out, out_shape=(jax.ShapeDtypeStruct((n_dp, own_rows...  1.47 us

profile of v2, /device:TPU:0, one launch (start us, length us, event | category | flops | bytes accessed | tf_op | source)
XLA Modules:
  0.0 32.2 jit_solution(16355709053620308015)
XLA Ops:
  1.9 0.6 %add_bitcast_fusion.counts = s32[1,2]{1,0:T(1,128)} fusion(s32[1]{0:T(128)S(6)} %copy.14, s32[1]{0:T(128)S(6)} %copy.13), kind=kLoop, calls=%fused_computation | loop fusion | flops 2 | bytes 16 | tf_op jit(solution)/shard_map/broadcast_in_dim | solution.py:306
  2.5 28.2 %shard_map.118 = (bf16[8,8,4096]{2,1,0:T(8,128)(2,1)S(1)}, f32[3,8,4096]{2,1,0:T(8,128)S(1)}, f32[2,1,128]{2,1,0:T(1,128)S(1)}) custom-call(f32[4,2,8,4096]{3,2,1,0:T(8,128)} %bitcast.11, s32[1,2]{1,0:T(1,128)} %add_bitcast_fusion.counts, f32[8,4096]{1,0:T(8,128)} %bitcast.12, f32[8,4096]{1,0:T(8,128)} %bitcast.13, f32[8,4096]{1,0:T(8,128)} %bitcast.14, ...), custom_call_target="tpu_custom_call" | custom-call | tf_op jit(solution)/shard_map/pallas_call | solution.py:267
  30.7 1.5 %shard_map.119 = (bf16[8,8,4096]{2,1,0:T(8,128)(2,1)}, f32[8,4096]{1,0:T(8,128)}, f32[8,4096]{1,0:T(8,128)}, f32[8,4096]{1,0:T(8,128)}, f32[1,8]{1,0:T(1,128)}, /*index=5*/f32[1,1]{1,0:T(1,128)}) custom-call(bf16[8,8,4096]{2,1,0:T(8,128)(2,1)S(1)} %get-tuple-element.15.params, f32[3,8,4096]{2,1,0:T(8,128)S(1)} %get-tuple-element.16.result, ...), custom_call_target="tpu_custom_call" | custom-call | tf_op jit(solution)/shard_map/pallas_call | solution.py:312

commit v3 on v2

--- a/solution.py
+++ b/solution.py
@@ -37,11 +37,12 @@
     n_dp,
     layers,
     grads,
-    counts,
+    skipped,
     master,
     moment_one,
     moment_two,
     bounds,
+    step,
     params,
     result,
     norms_out,
@@ -50,10 +51,8 @@
     paired,
     outgoing,
     incoming,
-    dp_stats,
-    section_stats,
+    stats,
     state,
-    counts_in,
     bounds_in,
     load_sem,
     pair_send,
@@ -62,8 +61,6 @@
     sum_recv,
     stat_send,
     stat_recv,
-    sec_send,
-    sec_recv,
     row_send,
     row_recv,
     near_send,
@@ -77,6 +74,7 @@
     partner = chip * PAIR + other
     own_rows, width = mine.shape[1], mine.shape[2]
     rows_all = n_dp * own_rows
+    place = section * n_dp + me
 
     def remote(src, dst, send, recv, sec, dp):
         return pltpu.make_async_remote_copy(
@@ -106,12 +104,7 @@
         pltpu.make_async_copy(source, state.at[k], load_sem.at[2 + k])
         for k, source in enumerate((master, moment_one, moment_two))
     ]
-    state_loads += [
-        pltpu.make_async_copy(source, target, load_sem.at[5 + k])
-        for k, (source, target) in enumerate(
-            ((counts, counts_in), (bounds, bounds_in))
-        )
-    ]
+    state_loads.append(pltpu.make_async_copy(bounds, bounds_in, load_sem.at[5]))
     for load in state_loads:
         load.start()
 
@@ -165,36 +158,32 @@
         high = jnp.where(lane == layer, bounds_in[0, layer + 1], high)
     inside = (row >= low) & (row < high)
     own_stats = jnp.sum(jnp.where(inside, row_squares, 0.0), axis=0, keepdims=True)
-    good = (MICRO - counts_in[0, 0]).astype(jnp.float32)
-    dp_stats[me] = jnp.where(lane == layers, good, own_stats)
-
-    def stat_copy(k):
-        return remote(
-            dp_stats.at[me], dp_stats.at[me], stat_send.at[k], stat_recv.at[k],
-            section, lax.rem(me + k + 1, n_dp),
-        )
-
-    repeat(n_dp - 1, lambda k: stat_copy(k).start())
-    step_value = jnp.full((1, 1), counts_in[0, 1], jnp.int32).astype(jnp.float32)
+    good = (MICRO - skipped[0]).astype(jnp.float32)
+    stats[place] = jnp.where(lane == layers, good, own_stats)
+
+    def stat_copy(ahead, k):
+        return remote(
+            stats.at[place], stats.at[place],
+            stat_send.at[ahead * n_dp + k], stat_recv.at[ahead * n_dp + k],
+            lax.rem(section + ahead, n_section), lax.rem(me + k, n_dp),
+        )
+
+    def each_peer(act):
+        for ahead in range(n_section - 1, 0, -1):
+            repeat(n_dp, lambda k: act(stat_copy(ahead, k)))
+        repeat(n_dp - 1, lambda k: act(stat_copy(0, k + 1)))
+
+    each_peer(lambda copy: copy.start())
+    step_value = jnp.full((1, 1), step[0], jnp.int32).astype(jnp.float32)
     fix_one = 1.0 - jnp.exp(step_value * math.log(beta_one))
     fix_two = 1.0 - jnp.exp(step_value * math.log(beta_two))
-    repeat(n_dp - 1, lambda k: stat_copy(k).wait_recv())
-    section_sum = jnp.sum(dp_stats[...], axis=0)
-    section_stats[section] = section_sum
-
-    def section_copy(k):
-        return remote(
-            section_stats.at[section], section_stats.at[section], sec_send.at[k], sec_recv.at[k],
-            lax.rem(section + k + 1, n_section), me,
-        )
-
-    repeat(n_section - 1, lambda k: section_copy(k).start())
+    layer_rows = jnp.where(lane < layers, high - low, 1).astype(jnp.float32)
+    each_peer(lambda copy: copy.wait_recv())
+    section_sum = jnp.sum(stats[pl.ds(section * n_dp, n_dp)], axis=0)
+    everything = jnp.sum(stats[...], axis=0)
     total_good = jnp.sum(jnp.where(lane == layers, section_sum, 0.0), axis=1, keepdims=True)
-    layer_rows = jnp.where(lane < layers, high - low, 1).astype(jnp.float32)
     norms = jnp.sqrt(section_sum / (layer_rows * width)) / total_good
     norms_out[0] = norms
-    repeat(n_section - 1, lambda k: section_copy(k).wait_recv())
-    everything = jnp.sum(section_stats[...], axis=0)
     total_sq = jnp.sum(jnp.where(lane < layers, everything, 0.0), axis=1, keepdims=True)
     grad_rms = jnp.sqrt(total_sq / (n_section * rows_all * width)) / total_good
     norms_out[1] = jnp.broadcast_to(grad_rms, (1, LANES))
@@ -232,8 +221,7 @@
     repeat(n_chip, lambda k: near_copy(k).wait_recv())
     repeat(n_chip, lambda k: pair_copy(k).wait_send())
     repeat(n_chip - 1, lambda k: sum_copy(k).wait_send())
-    repeat(n_dp - 1, lambda k: stat_copy(k).wait_send())
-    repeat(n_section - 1, lambda k: section_copy(k).wait_send())
+    each_peer(lambda copy: copy.wait_send())
     repeat(n_chip - 1, lambda k: row_copy(k).wait_send())
     repeat(n_chip, lambda k: near_copy(k).wait_send())
 
@@ -257,6 +245,7 @@
     own_rows = master.shape[1]
     layers = bounds.shape[1] - 1
     n_chip = n_dp // PAIR
+    smem = pl.BlockSpec(memory_space=pltpu.SMEM)
     hbm = pl.BlockSpec(memory_space=pltpu.HBM)
     held_bytes = rows_all * width * 2 + 3 * own_rows * width * 4 + SPARE
     vmem = pl.BlockSpec(memory_space=pltpu.VMEM)
@@ -271,7 +260,7 @@
             pltpu.VMEM((3, own_rows, width), jnp.float32),
             pltpu.VMEM((2, 1, LANES), jnp.float32),
         ),
-        in_specs=[hbm] * 6,
+        in_specs=[hbm, smem, hbm, hbm, hbm, hbm, smem],
         out_specs=(vmem, vmem, vmem),
         scratch_shapes=[
             blocks,
@@ -279,20 +268,16 @@
             blocks,
             halves,
             halves,
-            pltpu.VMEM((n_dp, 1, LANES), jnp.float32),
-            pltpu.VMEM((n_section, 1, LANES), jnp.float32),
+            pltpu.VMEM((n_section * n_dp, 1, LANES), jnp.float32),
             pltpu.VMEM((3, own_rows, width), jnp.float32),
-            pltpu.SMEM((1, 2), jnp.int32),
             pltpu.SMEM(bounds.shape, jnp.int32),
-            dma((7,)),
+            dma((6,)),
             dma((n_chip,)),
             dma((n_chip,)),
             dma((n_chip - 1,)),
             dma((n_chip - 1,)),
-            dma((n_dp - 1,)),
-            dma((n_dp - 1,)),
-            dma((n_section - 1,)),
-            dma((n_section - 1,)),
+            dma((n_section * n_dp,)),
+            dma((n_section * n_dp,)),
             dma((n_chip - 1,)),
             dma((n_chip - 1,)),
             dma((n_chip,)),
@@ -303,11 +288,12 @@
         ),
     )(
         grads.reshape(n_chip, PAIR, own_rows, width),
-        jnp.concatenate((skipped, step))[None],
+        skipped,
         master[0],
         moment_one[0],
         moment_two[0],
         bounds,
+        step,
     )
     params, master_next, first_next, second_next, layer_norms, grad_norm = pl.pallas_call(
         write_out,

time: 32.3 us -> 31 us (0.960)
  Pallas kernels: 29.6 us -> 29 us
  other arithmetic: 0.59 us -> 0 us
    pallas_call x1, Pallas kernels: 28.2 us -> 27.5 us  [on_device(): pl.pallas_call(functools.partial(kernel, n_section, n_dp, layers), out_sh...]
    broadcast_in_dim x1 -> x0, other arithmetic: 0.59 us -> none  [on_device(): jnp.concatenate((skipped, step))[None]]
where the time goes in v3:
time: 31 us; the launch traced here: 30.9 us
  Pallas kernels  29 us (94%)
  between operations  1.93 us (6%)
    pallas_call x1, Pallas kernels, on_device(): pl.pallas_call(functools.partial(kernel, n_section, n_dp, layers), out_sh...  27.5 us
    pallas_call x1, Pallas kernels, on_device(): pl.pallas_call(write_out, out_shape=(jax.ShapeDtypeStruct((n_dp, own_rows...  1.47 us

profile of v3, /device:TPU:0, one launch (start us, length us, event | category | flops | bytes accessed | tf_op | source)
XLA Modules:
  0.0 30.9 jit_solution(15302076114038662085)
XLA Ops:
  1.9 27.5 %shard_map.118 = (bf16[8,8,4096]{2,1,0:T(8,128)(2,1)S(1)}, f32[3,8,4096]{2,1,0:T(8,128)S(1)}, f32[2,1,128]{2,1,0:T(1,128)S(1)}) custom-call(f32[4,2,8,4096]{3,2,1,0:T(8,128)} %bitcast.9, s32[1]{0:T(128)S(6)} %copy.13.skipped, f32[8,4096]{1,0:T(8,128)} %bitcast.10, f32[8,4096]{1,0:T(8,128)} %bitcast.11, f32[8,4096]{1,0:T(8,128)} %bitcast.12, s32[1,9]{1,0:T(1,128)} %bounds.1, ...), custom_call_target="tpu_custom_call" | custom-call | tf_op jit(solution)/shard_map/pallas_call | solution.py:256
  29.4 1.5 %shard_map.119 = (bf16[8,8,4096]{2,1,0:T(8,128)(2,1)}, f32[8,4096]{1,0:T(8,128)}, f32[8,4096]{1,0:T(8,128)}, f32[8,4096]{1,0:T(8,128)}, f32[1,8]{1,0:T(1,128)}, /*index=5*/f32[1,1]{1,0:T(1,128)}) custom-call(bf16[8,8,4096]{2,1,0:T(8,128)(2,1)S(1)} %get-tuple-element.15.params, f32[3,8,4096]{2,1,0:T(8,128)S(1)} %get-tuple-element.16.result, ...), custom_call_target="tpu_custom_call" | custom-call | tf_op jit(solution)/shard_map/pallas_call | solution.py:298

commit v4 on v3

--- a/solution.py
+++ b/solution.py
@@ -84,6 +84,14 @@
 
     barrier = pltpu.get_barrier_semaphore()
 
+    def sweep(body):
+        if n_chip <= 8:
+            middle = n_chip // 2 - 1
+            for k in sorted(range(n_chip - 1), key=lambda k: k != middle):
+                body(k)
+        else:
+            repeat(n_chip - 1, body)
+
     def greet_dp(k):
         pl.semaphore_signal(
             barrier, inc=1, device_id=(section, lax.rem(me + k + 1, n_dp)), device_id_type=MESH
@@ -116,11 +124,9 @@
             theirs.at[z], paired.at[z], pair_send.at[off], pair_recv.at[off], section, partner
         )
 
-    def order(k):
-        return k + 1 if isinstance(k, int) and k + 1 < n_chip else lax.rem(k + 1, n_chip)
-
     load_theirs.wait()
-    repeat(n_chip, lambda k: pair_copy(order(k)).start())
+    sweep(lambda k: pair_copy(k + 1).start())
+    pair_copy(0).start()
     load_mine.wait()
 
     def sum_copy(k):
@@ -135,7 +141,7 @@
         outgoing[k] = (mine[z] + paired[z]).astype(jnp.bfloat16)
         sum_copy(k).start()
 
-    repeat(n_chip - 1, send_sum)
+    sweep(send_sum)
     pair_copy(0).wait_recv()
     mine[chip] = mine[chip] + paired[chip]
 
@@ -143,7 +149,7 @@
         sum_copy(k).wait_recv()
         mine[chip] = mine[chip] + incoming[k].astype(jnp.float32)
 
-    repeat(n_chip - 1, take_sum)
+    sweep(take_sum)
     total_grad = mine[chip]
 
     for load in state_loads:
@@ -207,7 +213,7 @@
             section, lax.rem(chip + k + 1, n_chip) * PAIR + core,
         )
 
-    repeat(n_chip - 1, lambda k: row_copy(k).start())
+    sweep(lambda k: row_copy(k).start())
     near_copy(0).start()
     result[0] = master_new
     result[1] = one
@@ -217,17 +223,20 @@
         row_copy(k).wait_recv()
         near_copy(n_chip - 1 - k).start()
 
-    repeat(n_chip - 1, pass_on)
-    repeat(n_chip, lambda k: near_copy(k).wait_recv())
     repeat(n_chip, lambda k: pair_copy(k).wait_send())
     repeat(n_chip - 1, lambda k: sum_copy(k).wait_send())
     each_peer(lambda copy: copy.wait_send())
+    sweep(pass_on)
+    repeat(n_chip, lambda k: near_copy(k).wait_recv())
     repeat(n_chip - 1, lambda k: row_copy(k).wait_send())
     repeat(n_chip, lambda k: near_copy(k).wait_send())
 
 
 def write_out(params, result, norms, params_out, master_next, first_next, second_next, layer_norms, grad_norm, sem):
-    copies = [pltpu.make_async_copy(params, params_out, sem.at[3])]
+    copies = [
+        pltpu.make_async_copy(params.at[k], params_out.at[k], sem.at[3 + k])
+        for k in range(params.shape[0])
+    ]
     copies += [
         pltpu.make_async_copy(result.at[k], target, sem.at[k])
         for k, target in enumerate((master_next, first_next, second_next))
@@ -307,7 +316,7 @@
         ),
         in_specs=[vmem] * 3,
         out_specs=(hbm, hbm, hbm, hbm, vmem, vmem),
-        scratch_shapes=[dma((4,))],
+        scratch_shapes=[dma((3 + n_dp,))],
         compiler_params=pltpu.CompilerParams(vmem_limit_bytes=SLACK),
     )(*held)
     return (

time: 31 us -> 30.9 us (level)
  no operation moved by 1% of the time
where the time goes in v4:
time: 30.9 us; the launch traced here: 30.8 us
  Pallas kernels  28.8 us (93%)
  between operations  1.93 us (6%)
    pallas_call x1, Pallas kernels, on_device(): pl.pallas_call(functools.partial(kernel, n_section, n_dp, layers), out_sh...  27.3 us
    pallas_call x1, Pallas kernels, on_device(): pl.pallas_call(write_out, out_shape=(jax.ShapeDtypeStruct((n_dp, own_rows...  1.53 us

profile of v4, /device:TPU:0, one launch (start us, length us, event | category | flops | bytes accessed | tf_op | source)
XLA Modules:
  0.0 30.8 jit_solution(9211572616747630080)
XLA Ops:
  1.9 27.3 %shard_map.118 = (bf16[8,8,4096]{2,1,0:T(8,128)(2,1)S(1)}, f32[3,8,4096]{2,1,0:T(8,128)S(1)}, f32[2,1,128]{2,1,0:T(1,128)S(1)}) custom-call(f32[4,2,8,4096]{3,2,1,0:T(8,128)} %bitcast.9, s32[1]{0:T(128)S(6)} %copy.13.skipped, f32[8,4096]{1,0:T(8,128)} %bitcast.10, f32[8,4096]{1,0:T(8,128)} %bitcast.11, f32[8,4096]{1,0:T(8,128)} %bitcast.12, s32[1,9]{1,0:T(1,128)} %bounds.1, ...), custom_call_target="tpu_custom_call" | custom-call | tf_op jit(solution)/shard_map/pallas_call | solution.py:265
  29.3 1.5 %shard_map.119 = (bf16[8,8,4096]{2,1,0:T(8,128)(2,1)}, f32[8,4096]{1,0:T(8,128)}, f32[8,4096]{1,0:T(8,128)}, f32[8,4096]{1,0:T(8,128)}, f32[1,8]{1,0:T(1,128)}, /*index=5*/f32[1,1]{1,0:T(1,128)}) custom-call(bf16[8,8,4096]{2,1,0:T(8,128)(2,1)S(1)} %get-tuple-element.15.params, f32[3,8,4096]{2,1,0:T(8,128)S(1)} %get-tuple-element.16.result, ...), custom_call_target="tpu_custom_call" | custom-call | tf_op jit(solution)/shard_map/pallas_call | solution.py:307
